TPU v7x, 32 devices: a 4x4x1 block of a 4x4x8 slice. The times are simulated.
32 devices in a mesh: dp: 1 (over z), ep: 32 (over y, x, core).
Axes of the slice: x: 4, y: 4, z: 1, core: 2. Of those that a mesh axis runs over, the one named last changes fastest.
The devices are a block of a 4x4x8 slice.
Arguments:
- resid_in: bfloat16 [4096, 2048], P(('dp', 'ep'))
- expert_ids: int32 [4096, 6], P(('dp', 'ep'))
- priority: int32 [4096, 6], P(('dp', 'ep'))
- norm_gain: float32 [2048], replicated
- router_w: bfloat16 [2048, 64], replicated
- shared_w1: bfloat16 [2048, 2816], replicated
- shared_w3: bfloat16 [2048, 2816], replicated
- shared_w2: bfloat16 [2816, 2048], replicated
- expert_w1: bfloat16 [64, 2048, 1408], P('ep')
- expert_w3: bfloat16 [64, 2048, 1408], P('ep')
- expert_w2: bfloat16 [64, 1408, 2048], P('ep')
Outputs:
- output: bfloat16 [4096, 2048], P(('dp', 'ep'))
All inputs are finite; a program needn't handle non-finite values.
Results may differ from a plain program's by a relative error of at most 0.00677691.
Values are sent between devices in bfloat16 or wider.
A program may use at most 768 MiB of HBM per device.

v0:
```python
import functools
import math

import jax
import jax.numpy as jnp
from jax import lax
from jax.experimental import pallas as pl
from jax.experimental.pallas import tpu as pltpu
from jax.sharding import PartitionSpec as P

NORM_EPS = 1e-6
ROUTE_SCALE = 16.0
MESH = pl.DeviceIdType.MESH
F32 = jnp.float32
BF16 = jnp.bfloat16
PAIR = (0, 1)
SPLIT = (2, 3)
SENDS = SPLIT + PAIR
LANES = (((1,), (1,)), ((), ()))
FAR = 1 << 20
TILE = 128
PARTS = ((0, 512), (512, 1024))
AHEAD = 2
CAP = 72
VMEM_LIMIT = 64000 * 1024


class Place:
    def __init__(self, ep):
        self.side = math.isqrt(ep // 2)
        self.me = lax.axis_index("ep")
        self.core = lax.rem(self.me, 2)
        self.chip = self.me // 2
        self.px = lax.rem(self.chip, self.side)
        self.py = self.chip // self.side
        self.partner = self.me + 1 - 2 * self.core

    def dev(self, dx, dy, core=None):
        x = lax.rem(self.px + dx % self.side, self.side)
        y = lax.rem(self.py + dy % self.side, self.side)
        return (y * self.side + x) * 2 + (self.core if core is None else core)

    def at(self, fam, du, dv, core=None):
        return self.dev(du, dv, core) if fam == 0 else self.dev(dv, du, core)


def loop(n, body, start=0, unroll=1):
    def step(i, carry):
        body(i)
        return carry

    lax.fori_loop(start, n, step, 0, unroll=unroll)


def iota(shape, axis):
    return lax.broadcasted_iota(jnp.int32, shape, axis)


def tri(n, m, rows_first):
    i = iota((n, m), 0)
    j = iota((n, m), 1)
    return jnp.where(i < j if rows_first else j < i, 1.0, 0.0).astype(BF16)


def mm(a, b):
    return jnp.dot(a.astype(BF16), b.astype(BF16), preferred_element_type=F32)


def mm_t(a, b):
    return lax.dot_general(a.astype(BF16), b.astype(BF16), LANES, preferred_element_type=F32)


def route(pc, ep, top_k, n_local, n_chips, meta_all, ids, prs, pr, thr, cnt, kch, pos, ka, kb, info_ref, q_ref):
    n_exp = ep * n_local
    tok = ids.shape[2]
    capacity = tok * top_k
    n_bits = (ep * capacity).bit_length()

    def unpack(s):
        for k in range(top_k):
            ids[k, pl.ds(s, 1), :] = meta_all[s, k : k + 1, :]
            prs[k, pl.ds(s, 1), :] = meta_all[s, top_k + k : top_k + k + 1, :]

    loop(ep, unpack)

    def per_expert(e):
        best = jnp.full((ep, tok), FAR, jnp.int32)
        for k in range(top_k):
            best = jnp.minimum(best, jnp.where(ids[k] == e, prs[k], FAR))
        pr[e] = best

    loop(n_exp, per_expert)

    thr[...] = jnp.zeros(thr.shape, jnp.int32)

    def bit_step(i, step):
        for d in range(ep):
            cand = thr[d : d + 1, :] + step
            hits = jnp.zeros((ep, tok), F32)
            for l in range(n_local):
                hits = hits + jnp.where(pr[d * n_local + l] < cand, 1.0, 0.0)
            cnt[d : d + 1, :] = jnp.sum(hits, axis=0, keepdims=True)
        total = jnp.sum(cnt[...], axis=1, keepdims=True)
        thr[...] = thr[...] + jnp.where(total <= capacity, step, 0)
        return step // 2

    lax.fori_loop(0, n_bits, bit_step, jnp.int32(1 << (n_bits - 1)))

    def chip_counts(d):
        kept = jnp.zeros((ep, tok), F32)
        for l in range(n_local):
            kept = kept + jnp.where(pr[d * n_local + l] < thr[pl.ds(d, 1), :], 1.0, 0.0)
        kch[pl.ds(pl.multiple_of(d * ep, ep), ep), :] = kept

    loop(ep, chip_counts)
    pairs = kch[pl.ds(0, ep * n_chips, stride=2), :] + kch[pl.ds(1, ep * n_chips, stride=2), :]
    worst = jnp.max(jnp.sum(pairs, axis=1, keepdims=True), axis=0, keepdims=True)
    info_ref[...] = jnp.broadcast_to(worst, info_ref.shape).astype(jnp.int32)
    upper = tri(tok, tok, True)
    ones = jnp.ones((tok, tok), BF16)
    lower = tri(ep, ep, False)
    my_thr = thr[pl.ds(pc.me, 1), :]
    base = jnp.zeros((1, tok), F32)
    for l in range(n_local):
        kept = pr[pc.me * n_local + l] < my_thr
        kept_f = jnp.where(kept, 1.0, 0.0)
        in_row = mm(kept_f, upper)
        row_total = mm(kept_f, ones)
        row_start = mm(lower, row_total)
        pos[l] = jnp.where(kept, (in_row + row_start + base), -1.0).astype(jnp.int32)
        totals = mm_t(jnp.ones((8, tok), F32), kept_f)
        starts = mm(totals, tri(ep, ep, True)) + base[:, :ep]
        info_ref[2 * l : 2 * l + 1, :ep] = totals[:1].astype(jnp.int32)
        info_ref[2 * l + 1 : 2 * l + 2, :ep] = starts[:1].astype(jnp.int32)
        group = jnp.sum(row_total, axis=0, keepdims=True)
        base = base + jnp.floor((group + (TILE - 1)) * (1.0 / TILE)) * TILE

    def chip_rows(e):
        limit = thr[pl.ds(e // n_local, 1), :]
        first = pr[e, pl.ds(pc.chip * 2, 1), :]
        second = pr[e, pl.ds(pc.chip * 2 + 1, 1), :]
        ka[pl.ds(e, 1), :] = jnp.where(first < limit, 1.0, 0.0)
        kb[pl.ds(e, 1), :] = jnp.where(second < limit, 1.0, 0.0)

    loop(n_exp, chip_rows)
    k_a, k_b = ka[...], kb[...]
    tot_a = mm(k_a, ones)
    both = tot_a + mm(k_b, ones)
    i = iota((n_exp, n_exp), 0)
    j = iota((n_exp, n_exp), 1)
    earlier = jnp.where((j < i) & (j // n_local == i // n_local), 1.0, 0.0)
    before = mm(earlier, both)
    q_a = jnp.where(k_a > 0, mm(k_a, upper) + before, -1.0)
    q_b = jnp.where(k_b > 0, mm(k_b, upper) + tot_a + before, -1.0)
    second_core = iota(q_ref.shape, 0) * 0 + pc.core
    q_ref[...] = jnp.where(second_core == 0, q_a, q_b).astype(jnp.int32)


def dispatch_kernel(
    ep, top_k, n_local, y_ref, ids_ref, prio_ref, gain_ref, router_ref, sw1_hbm, sw3_hbm, sw2_hbm,
    x_hbm, info_ref, q_ref, gate_ref, base_ref,
    x_ref, b_ref, meta_ref, yall, meta_all, ids, prs, pr, thr, cnt, kch, pos, ka, kb, sel, sw1, sw3, sw2,
    own_sem, x_sem, sw_sem, m_send, m_recv, s_send, s_recv, p_send, p_recv, o_send, o_recv,
):
    pc = Place(ep)
    side, me = pc.side, pc.me
    tok, dim = y_ref.shape
    half, quarter, n_chips = tok // 2, tok // 4, ep // 2
    n_buf, width = sw1.shape[0], sw1.shape[2]
    n_chunks = sw1_hbm.shape[1] // width

    def shared_loads(c):
        slot = lax.rem(c, n_buf)
        cols = pl.ds(pl.multiple_of(c * width, width), width)
        return [
            pltpu.make_async_copy(sw1_hbm.at[:, cols], sw1.at[slot], sw_sem.at[slot, 0]),
            pltpu.make_async_copy(sw3_hbm.at[:, cols], sw3.at[slot], sw_sem.at[slot, 1]),
            pltpu.make_async_copy(sw2_hbm.at[cols, :], sw2.at[slot], sw_sem.at[slot, 2]),
        ]

    def first_loads(c):
        for load in shared_loads(c):
            load.start()

    loop(n_buf, first_loads)

    meta_ref[0:top_k, :] = ids_ref[...]
    meta_ref[top_k:, :] = prio_ref[...]

    def norm(i):
        rows = pl.ds(pl.multiple_of(i * 16, 16), 16)
        y = y_ref[rows, :].astype(F32)
        inv_rms = lax.rsqrt(jnp.mean(y * y, axis=1, keepdims=True) + NORM_EPS)
        b_ref[rows, :] = (y * inv_rms * gain_ref[...]).astype(BF16)

    loop(tok // 16, norm)

    barrier = pltpu.get_barrier_semaphore()

    def greet(o):
        pl.semaphore_signal(barrier, inc=1, device_id={"ep": lax.rem(me + 2 * o, ep)}, device_id_type=MESH)

    loop(n_chips, greet, 1)
    pl.semaphore_signal(barrier, inc=1, device_id={"ep": pc.partner}, device_id_type=MESH)
    pl.semaphore_wait(barrier, n_chips)

    own = pltpu.make_async_copy(b_ref, yall.at[me], own_sem)
    own.start()

    def meta_copy(o, src):
        return pltpu.make_async_remote_copy(
            src_ref=meta_ref, dst_ref=meta_all.at[src], send_sem=m_send.at[o], recv_sem=m_recv.at[o],
            device_id={"ep": lax.rem(me + 2 * o, ep)}, device_id_type=MESH,
        )

    def meta_pass(o, origin, src=None):
        block = lax.rem(origin - 2 * o + ep, ep)
        return pltpu.make_async_remote_copy(
            src_ref=meta_all.at[block] if src is None else src, dst_ref=meta_all.at[block],
            send_sem=m_send.at[n_chips + o], recv_sem=m_recv.at[n_chips + o], device_id={"ep": pc.partner}, device_id_type=MESH,
        )

    def send_meta(o):
        meta_copy(o, me).start()

    loop(n_chips, send_meta, 1)
    meta_pass(0, me, meta_ref).start()

    def piece(fam, g, k, sent):
        j = g - 1
        hop = -1 if k % 2 else 1
        dist = (0 if sent else -hop) if k in PAIR else (-hop if sent else 2)
        du, dv = (dist, 0) if g == 0 else (j, dist)
        start = fam * half + (quarter if k == 3 else 0)
        size = half if k < 2 else quarter
        return du % side, dv % side, start, size, hop

    def link_copy(fam, g, k, sent):
        du, dv, start, size, hop = piece(fam, g, k, sent)
        block = pc.at(fam, du, dv)
        rows = yall.at[block, pl.ds(start, size), :]
        source = b_ref.at[pl.ds(start, size), :] if sent and (du, dv) == (0, 0) else rows
        target = pc.at(fam, hop, 0) if g == 0 else pc.at(fam, 0, hop)
        n = (fam * (side + 1) + g) * 4 + k
        return pltpu.make_async_remote_copy(
            src_ref=source, dst_ref=rows, send_sem=s_send.at[n], recv_sem=s_recv.at[n], device_id={"ep": target}, device_id_type=MESH
        )

    def pass_on(fam, g, k, mine):
        du, dv, start, size, _ = piece(fam, g, k, False)
        block = pc.at(fam, du, dv, pc.core if mine else 1 - pc.core)
        rows = yall.at[block, pl.ds(start, size), :]
        n = (fam * (side + 1) + g) * 4 + k
        return pltpu.make_async_remote_copy(
            src_ref=rows, dst_ref=rows, send_sem=p_send.at[n], recv_sem=p_recv.at[n], device_id={"ep": pc.partner}, device_id_type=MESH
        )

    def own_to_partner(block):
        return pltpu.make_async_remote_copy(
            src_ref=b_ref, dst_ref=yall.at[block], send_sem=o_send, recv_sem=o_recv, device_id={"ep": pc.partner}, device_id_type=MESH
        )

    for fam in PAIR:
        for k in PAIR:
            link_copy(fam, 0, k, True).start()
    own_to_partner(me).start()
    for fam in PAIR:
        for k in PAIR:
            link_copy(fam, 1, k, True).start()

    def wait_meta(o):
        meta_copy(o, lax.rem(me - 2 * o + ep, ep)).wait_recv()
        meta_pass(o, me).start()

    def wait_passed(o):
        meta_pass(o, pc.partner).wait_recv()

    def gates():
        logits = lax.dot_general(router_ref[...], b_ref[...], LANES, preferred_element_type=F32)
        probs = jnp.exp(logits - jnp.max(logits, axis=0, keepdims=True))
        gate_ref[...] = ROUTE_SCALE * (probs / jnp.sum(probs, axis=0, keepdims=True))

    def shared(c):
        slot = lax.rem(c, n_buf)
        for load in shared_loads(c):
            load.wait()
        up_a = jnp.dot(b_ref[...], sw1[slot], preferred_element_type=F32)
        up_b = jnp.dot(b_ref[...], sw3[slot], preferred_element_type=F32)
        act = (up_a * jax.nn.sigmoid(up_a) * up_b).astype(BF16)
        base_ref[...] += jnp.dot(act, sw2[slot], preferred_element_type=F32)

        @pl.when(c + n_buf < n_chunks)
        def _():
            for load in shared_loads(c + n_buf):
                load.start()

    base_ref[...] = jnp.zeros(base_ref.shape, F32)
    shared_done = [0]

    def fill_in(n):
        end = min(shared_done[0] + n, n_chunks)
        if end > shared_done[0]:
            loop(end, shared, shared_done[0])
        shared_done[0] = end

    meta_all[me] = meta_ref[...]
    gates()
    loop(n_chips, wait_meta, 1)
    loop(n_chips, wait_passed)
    route(pc, ep, top_k, n_local, n_chips, meta_all, ids, prs, pr, thr, cnt, kch, pos, ka, kb, info_ref, q_ref)

    slots = x_ref.shape[0]
    n_cols = 512
    lane = iota((1, tok), 1)

    def pick(halves, first=False):
        depth = len(halves) * tok
        where_to = [[jnp.where(lane < half, pos[l, pl.ds(lo, 1), :], pos[l, pl.ds(hi, 1), :]) for l in range(n_local)] for lo, hi in halves]

        def build(i):
            rows = pl.ds(pl.multiple_of(i * TILE, TILE), TILE)
            slot = iota((TILE, tok), 0) + i * TILE
            for n, places in enumerate(where_to):
                hit = slot == places[0]
                for place in places[1:]:
                    hit = hit | (slot == place)
                sel[rows, n * tok : (n + 1) * tok] = jnp.where(hit, 1.0, 0.0).astype(BF16)

        loop(slots // TILE, build)

        def one(n):
            cols = pl.ds(pl.multiple_of(n * n_cols, n_cols), n_cols)
            pieces = []
            for lo, hi in halves:
                pieces += [yall[lo, :half, cols], yall[hi, half:, cols]]
            picked = jnp.dot(sel[:, :depth], jnp.concatenate(pieces, axis=0), preferred_element_type=F32).astype(BF16)
            x_ref[:, cols] = picked if first else x_ref[:, cols] + picked

        loop(dim // n_cols, one)

    def two(ks):
        return [(f, k) for f in PAIR for k in ks]

    steps = [(0, PAIR), (1, PAIR), (0, SPLIT), (side, PAIR), (2, PAIR), (1, SPLIT), (3, PAIR)]
    steps += [(g, SPLIT) for g in (side, 2, 3)]

    def receive(g, ks):
        for f, k in two(ks):
            link_copy(f, g, k, False).wait_recv()
            if k < 2:
                link_copy(f, g, k + 2, True).start()
        if g == 0:
            for j in (side - 1, 1) if ks == PAIR else (2,):
                for f, k in two(PAIR):
                    link_copy(f, 1 + j, k, True).start()
        for f, k in two(ks):
            pass_on(f, g, k, True).start()

    def take(g, ks):
        for f, k in two(ks):
            pass_on(f, g, k, False).wait_recv()
        halves = []
        for k in ks if ks == PAIR else (2,):
            for core in (pc.core, 1 - pc.core):
                halves.append(tuple(pc.at(f, *piece(f, g, k, False)[:2], core) for f in PAIR))
        pick(halves)

    own.wait()
    own_to_partner(pc.partner).wait_recv()
    pick([(me, me), (pc.partner, pc.partner)], first=True)
    for i, step in enumerate(steps):
        receive(*step)
        if i > 0:
            take(*steps[i - 1])
        if i in (1, 3, 4, 6):
            fill_in(3)
    take(*steps[-1])
    x_out = pltpu.make_async_copy(x_ref, x_hbm, x_sem)
    x_out.start()
    base_ref[...] = y_ref[...].astype(F32) + base_ref[...].astype(BF16).astype(F32)

    def sent_meta(o):
        meta_copy(o, me).wait_send()
        meta_pass(o, me).wait_send()

    loop(n_chips, sent_meta, 1)
    meta_pass(0, me, meta_ref).wait_send()
    own_to_partner(me).wait_send()
    for g, ks in steps:
        for f, k in two(ks):
            link_copy(f, g, k, True).wait_send()
            pass_on(f, g, k, True).wait_send()
    x_out.wait()


def dispatch(ep, n_local, resid_in, expert_ids, priority, norm_gain, router_w, shared_w1, shared_w3, shared_w2):
    tok, dim = resid_in.shape
    top_k = expert_ids.shape[1]
    side = math.isqrt(ep // 2)
    n_exp = ep * n_local
    slots = tok * top_k + (n_local - 1) * TILE
    n_piece = 2 * (side + 1) * 4
    n_buf, width = 3, 256
    vmem = pl.BlockSpec(memory_space=pltpu.VMEM)
    hbm = pl.BlockSpec(memory_space=pl.ANY)
    dma = pltpu.SemaphoreType.DMA
    return pl.pallas_call(
        functools.partial(dispatch_kernel, ep, top_k, n_local),
        out_shape=(
            jax.ShapeDtypeStruct((slots, dim), BF16),
            jax.ShapeDtypeStruct((8, 128), jnp.int32),
            jax.ShapeDtypeStruct((n_exp, tok), jnp.int32),
            jax.ShapeDtypeStruct((n_exp, tok), F32),
            jax.ShapeDtypeStruct((tok, dim), F32),
        ),
        in_specs=[vmem] * 5 + [hbm] * 3,
        out_specs=(hbm, vmem, vmem, vmem, vmem),
        scratch_shapes=[
            pltpu.VMEM((slots, dim), BF16),
            pltpu.VMEM((tok, dim), BF16),
            pltpu.VMEM((2 * top_k, tok), jnp.int32),
            pltpu.VMEM((ep, tok, dim), BF16),
            pltpu.VMEM((ep, 2 * top_k, tok), jnp.int32),
            pltpu.VMEM((top_k, ep, tok), jnp.int32),
            pltpu.VMEM((top_k, ep, tok), jnp.int32),
            pltpu.VMEM((n_exp, ep, tok), jnp.int32),
            pltpu.VMEM((ep, tok), jnp.int32),
            pltpu.VMEM((ep, tok), F32),
            pltpu.VMEM((ep * ep, tok), F32),
            pltpu.VMEM((n_local, ep, tok), jnp.int32),
            pltpu.VMEM((n_exp, tok), F32),
            pltpu.VMEM((n_exp, tok), F32),
            pltpu.VMEM((slots, 4 * tok), BF16),
            pltpu.VMEM((n_buf, dim, width), BF16),
            pltpu.VMEM((n_buf, dim, width), BF16),
            pltpu.VMEM((n_buf, width, dim), BF16),
            dma(()), dma(()), dma((n_buf, 3)),
            dma((ep,)), dma((ep,)), dma((n_piece,)), dma((n_piece,)), dma((n_piece,)), dma((n_piece,)), dma(()), dma(()),
        ],
        compiler_params=pltpu.CompilerParams(collective_id=0, has_side_effects=True, vmem_limit_bytes=VMEM_LIMIT),
        name="dispatch",
    )(
        resid_in, expert_ids.T, priority.T, norm_gain.reshape(1, dim), router_w.T, shared_w1, shared_w3, shared_w2,
    )


def expert_kernel(
    ep, sc, x_hbm, w1_hbm, w3_hbm, w2_hbm, e_hbm, a_hbm, b_hbm, x_ref, e_ref, act, w1, w3, w2, bk, x_sem, e_sem, sems, bk_sem
):
    n_local, dim, ff = w1.shape
    slots = x_ref.shape[0]
    step = 4 * TILE
    parts = PARTS + ((PARTS[-1][1], ff),)
    last = len(parts)
    x_in = pltpu.make_async_copy(x_hbm, x_ref, x_sem)

    def loads(l, n):
        if n == last:
            return [pltpu.make_async_copy(w2_hbm.at[l], w2.at[l], sems.at[l, 2 * n])]
        cols = pl.ds(parts[n][0], parts[n][1] - parts[n][0])
        return [
            pltpu.make_async_copy(w_hbm.at[l, :, cols], w.at[l, :, cols], sems.at[l, 2 * n + i])
            for i, (w_hbm, w) in enumerate(((w1_hbm, w1), (w3_hbm, w3)))
        ]

    def request(l, n):
        l, n = (l, n) if n <= last else (l + 1, n - last - 1)

        @pl.when(l < n_local)
        def _():
            for load in loads(l, n):
                load.start()

    def arrive(l, n):
        for load in loads(l, n):
            load.wait()
        request(l, n + AHEAD)

    x_in.start()
    for n in range(AHEAD):
        request(0, n)

    def over_tiles(first, count, body):
        most = 4
        whole = count // most

        def many(i):
            body(pl.ds(pl.multiple_of((first + i * most) * TILE, TILE), most * TILE))

        loop(whole, many)
        for rest in range(1, most):

            @pl.when(lax.rem(count, most) == rest)
            def _():
                body(pl.ds(pl.multiple_of((first + whole * most) * TILE, TILE), rest * TILE))

    x_in.wait()

    def one_expert(l, done):
        count = (sc[2 * l + 1, ep - 1] - sc[2 * l + 1, 0] + sc[2 * l, ep - 1] + TILE - 1) // TILE

        def up_cols(n):
            start = pl.multiple_of(jnp.minimum(n * step, ff - step), TILE)
            for p, (c, _) in enumerate(parts):

                @pl.when(n * step == c)
                def _():
                    arrive(l, p)

            def up(rows):
                x = x_ref[rows, :]
                up_a = jnp.dot(x, w1[l, :, pl.ds(start, step)], preferred_element_type=F32)
                up_b = jnp.dot(x, w3[l, :, pl.ds(start, step)], preferred_element_type=F32)
                act[rows, pl.ds(start, step)] = (up_a * jax.nn.sigmoid(up_a) * up_b).astype(BF16)

            over_tiles(done, count, up)

        loop(-(-ff // step), up_cols)
        arrive(l, last)

        def down_cols(n):
            cols = pl.ds(pl.multiple_of(n * step, step), step)

            def down(rows):
                e_ref[rows, cols] = jnp.dot(act[rows, :], w2[l, :, cols], preferred_element_type=F32).astype(BF16)

            over_tiles(done, count, down)

        loop(dim // step, down_cols)
        return done + count

    done = lax.fori_loop(0, n_local, one_expert, 0)

    def clear(i):
        rows = pl.ds(pl.multiple_of(i * TILE, TILE), TILE)
        e_ref[rows, :] = jnp.zeros((TILE, dim), BF16)

    loop(slots // TILE, clear, done)
    e_out = pltpu.make_async_copy(e_ref, e_hbm, e_sem)
    e_out.start()
    fill_buckets(ep, sc, 0, e_ref, a_hbm, b_hbm, bk, bk_sem, n_local)
    e_out.wait()


def bucket_shape(ep, dim):
    side = math.isqrt(ep // 2)
    return jax.ShapeDtypeStruct((side, 2, side, CAP, dim // 4), BF16)


def bucket_scratch(ep, dim):
    n_chips = ep // 2
    return [pltpu.VMEM((n_chips, 4, CAP, dim // 4), BF16), pltpu.SemaphoreType.DMA((n_chips, 4))]


def experts(ep, info, x, expert_w1, expert_w3, expert_w2):
    hbm = pl.BlockSpec(memory_space=pl.ANY)
    n_local, dim, ff = expert_w1.shape
    bucket = bucket_shape(ep, dim)
    bk, bk_sem = bucket_scratch(ep, dim)
    dma = pltpu.SemaphoreType.DMA
    return pl.pallas_call(
        functools.partial(expert_kernel, ep),
        out_shape=(jax.ShapeDtypeStruct(x.shape, BF16), bucket, bucket),
        in_specs=[pl.BlockSpec(memory_space=pltpu.SMEM)] + [hbm] * 4,
        out_specs=(hbm, hbm, hbm),
        scratch_shapes=[
            pltpu.VMEM(x.shape, BF16),
            pltpu.VMEM(x.shape, BF16),
            pltpu.VMEM((x.shape[0], ff), BF16),
            pltpu.VMEM((n_local, dim, ff), BF16),
            pltpu.VMEM((n_local, dim, ff), BF16),
            pltpu.VMEM((n_local, ff, dim), BF16),
            bk, dma(()), dma(()), dma((n_local, 2 * len(PARTS) + 3)), bk_sem,
        ],
        compiler_params=pltpu.CompilerParams(vmem_limit_bytes=VMEM_LIMIT),
        name="experts",
    )(info, x, expert_w1, expert_w3, expert_w2)


def fill_kernel(ep, n_local, sc, rnd, e_ref, a_hbm, b_hbm, bk, bk_sem):
    fill_buckets(ep, sc, rnd[0], e_ref, a_hbm, b_hbm, bk, bk_sem, n_local)


def fill_buckets(ep, sc, rnd, e_ref, a_hbm, b_hbm, bk, bk_sem, n_local):
    pc = Place(ep)
    side = pc.side
    slots, dim = e_ref.shape
    width = dim // 4
    pack = 16
    window = (CAP + 2 * pack - 2) // pack * pack
    skip = rnd * CAP

    def out_copies(n):
        dx, dy = lax.rem(n, side), n // side
        targets = [a_hbm.at[dx, c, dy] for c in PAIR] + [b_hbm.at[dy, c, dx] for c in PAIR]
        return [pltpu.make_async_copy(bk.at[n, c], target, bk_sem.at[n, c]) for c, target in enumerate(targets)]

    def one(n):
        dx, dy = lax.rem(n, side), n // side
        chip = lax.rem(pc.py + dy, side) * side + lax.rem(pc.px + dx, side)
        row = iota((CAP, window), 0)
        col = iota((CAP, window), 1)
        out = jnp.zeros((CAP, dim), F32)
        lead = -skip
        for l in range(n_local):
            start, count = sc[2 * l + 1, 2 * chip], sc[2 * l, 2 * chip] + sc[2 * l, 2 * chip + 1]
            used = jnp.minimum(jnp.maximum(-lead, 0), count)
            origin = jnp.minimum((start + used) // pack * pack, slots - window)
            origin = pl.multiple_of(origin, pack)
            slot = row - lead + start
            hit = (slot == col + origin) & (row >= lead) & (row < lead + count)
            out = out + jnp.dot(jnp.where(hit, 1.0, 0.0).astype(BF16), e_ref[pl.ds(origin, window), :], preferred_element_type=F32)
            lead = lead + count
        out = out.astype(BF16)
        for c, copy in enumerate(out_copies(n)):
            bk[n, c] = out[:, c * width : (c + 1) * width]
            copy.start()

    def sent(n):
        for copy in out_copies(n):
            copy.wait()

    loop(side * side, one, unroll=4)
    loop(side * side, sent)


def fill(ep, n_local, info, rnd, e):
    vmem = pl.BlockSpec(memory_space=pltpu.VMEM)
    smem = pl.BlockSpec(memory_space=pltpu.SMEM)
    hbm = pl.BlockSpec(memory_space=pl.ANY)
    bucket = bucket_shape(ep, e.shape[1])
    return pl.pallas_call(
        functools.partial(fill_kernel, ep, n_local),
        out_shape=(bucket, bucket),
        in_specs=[smem, smem, vmem],
        out_specs=(hbm, hbm),
        scratch_shapes=bucket_scratch(ep, e.shape[1]),
        compiler_params=pltpu.CompilerParams(vmem_limit_bytes=VMEM_LIMIT),
        name="fill",
    )(info, rnd, e)


def combine_kernel(
    ep, n_local, a_hbm, b_hbm, q_ref, p_ref, acc_ref, out_ref, bk, st, rl, fin, ry, pf, g_ref, bk_sem, s_send, s_recv, p_send, p_recv
):
    pc = Place(ep)
    side = pc.side
    tok = q_ref.shape[1]
    width = bk.shape[-1]
    loads = [pltpu.make_async_copy(src, bk.at[fam], bk_sem.at[fam]) for fam, src in enumerate((a_hbm, b_hbm))]
    for load in loads:
        load.start()

    barrier = pltpu.get_barrier_semaphore()
    friends = [pc.dev(1, 0), pc.dev(-1, 0), pc.dev(0, 1), pc.dev(0, -1), pc.partner]
    for friend in friends:
        pl.semaphore_signal(barrier, inc=1, device_id={"ep": friend}, device_id_type=MESH)
    pl.semaphore_wait(barrier, len(friends))
    for load in loads:
        load.wait()

    ring = (0, 1, side - 1, 2)

    def held(fam, j):
        return bk.at[fam, 0] if j == 0 else st.at[fam, j]

    def link_copy(fam, g, k):
        hop = 1 if k % 2 == 0 else -1
        c = k % 2
        if g == 0:
            target = pc.at(fam, hop, 0)
            if k < 2:
                src, dst = bk.at[fam, hop % side], st.at[fam, hop % side]
            elif k < 4:
                src, dst = bk.at[fam, 2, c], rl.at[fam, c]
            else:
                src, dst = rl.at[fam, c], st.at[fam, 2, c]
        else:
            j = g - 1
            target = pc.at(fam, 0, hop)
            if k < 2:
                src, dst = held(fam, j).at[:, hop % side], fin.at[fam, j, hop % side]
            elif k < 4:
                src, dst = held(fam, j).at[c, 2], ry.at[fam, j, c]
            else:
                src, dst = ry.at[fam, j, c], fin.at[fam, j, 2, c]
        n = (fam * (side + 1) + g) * 6 + k
        return pltpu.make_async_remote_copy(
            src_ref=src, dst_ref=dst, send_sem=s_send.at[n], recv_sem=s_recv.at[n], device_id={"ep": target}, device_id_type=MESH
        )

    def arrived(fam, j, v):
        return held(fam, j).at[:, 0] if v == 0 else fin.at[fam, j, v]

    def pass_on(fam, j, v):
        n = (fam * side + j) * side + v
        return pltpu.make_async_remote_copy(
            src_ref=arrived(fam, j, v), dst_ref=pf.at[fam, j, v], send_sem=p_send.at[n], recv_sem=p_recv.at[n],
            device_id={"ep": pc.partner}, device_id_type=MESH,
        )

    for k in SENDS:
        for fam in PAIR:
            link_copy(fam, 0, k).start()
    for k in SENDS:
        for fam in PAIR:
            link_copy(fam, 1, k).start()
    for fam in PAIR:
        pass_on(fam, 0, 0).start()

    row = iota((g_ref.shape[3], tok), 0)

    def weights(d):
        w = jnp.zeros(row.shape, F32)
        for l in range(n_local):
            e = d * n_local + l
            w = w + jnp.where(row == q_ref[pl.ds(e, 1), :], p_ref[pl.ds(e, 1), :], 0.0)
        w = w.T
        for n in range(3):
            term = w.astype(BF16)
            g_ref[d, n] = term
            w = w - term.astype(F32)

    loop(ep, weights)
    out_ref[...] = acc_ref[...]

    def add(fam, j, v):
        devs = [pc.at(fam, -j, -v), pc.at(fam, -j, -v, 1 - pc.core)]

        def one(c):
            cols = pl.ds(pl.multiple_of((2 * fam + c) * width, width), width)
            total = out_ref[:, cols]
            for d, rows in zip(devs, (arrived(fam, j, v), pf.at[fam, j, v])):
                data = rows[c]
                for n in range(3):
                    total = total + jnp.dot(g_ref[d, n][:, :CAP], data, preferred_element_type=F32)
            out_ref[:, cols] = total

        loop(2, one, unroll=2)

    ready = []

    def here(fam, j, v):
        pass_on(fam, j, v).start()
        ready.append((fam, j, v))

    def drain(keep):
        while len(ready) > keep:
            fam, j, v = ready.pop(0)
            pass_on(fam, j, v).wait_recv()
            add(fam, j, v)

    def got(fam, g, k):
        link_copy(fam, g, k).wait_recv()

    ready += [(0, 0, 0), (1, 0, 0)]
    for k in SPLIT:
        for fam in PAIR:
            got(fam, 0, k)
            link_copy(fam, 0, k + 2).start()
    drain(0)
    for k in PAIR:
        for fam in PAIR:
            got(fam, 0, k)
            j = 1 if k == 0 else side - 1
            for kk in SENDS:
                link_copy(fam, 1 + j, kk).start()
            here(fam, j, 0)
    for k in SPLIT:
        for fam in PAIR:
            got(fam, 1, k)
            link_copy(fam, 1, k + 2).start()
    for fam in PAIR:
        got(fam, 0, 4)
        got(fam, 0, 5)
        for kk in SENDS:
            link_copy(fam, 3, kk).start()
        here(fam, 2, 0)
    drain(2)
    for j in ring:
        if j > 0:
            for k in SPLIT:
                for fam in PAIR:
                    got(fam, 1 + j, k)
                    link_copy(fam, 1 + j, k + 2).start()
        for k in PAIR:
            for fam in PAIR:
                got(fam, 1 + j, k)
                here(fam, j, 1 if k == 0 else side - 1)
        drain(2)
    for j in ring:
        for fam in PAIR:
            got(fam, 1 + j, 4)
            got(fam, 1 + j, 5)
            here(fam, j, 2)
        drain(4)
    drain(0)
    for fam in PAIR:
        for g in range(side + 1):
            for k in range(6):
                link_copy(fam, g, k).wait_send()
        for j in range(side):
            for v in range(side):
                pass_on(fam, j, v).wait_send()


def combine(ep, n_local, bka, bkb, q, weights, acc):
    side = math.isqrt(ep // 2)
    cap, width = bka.shape[-2:]
    tok = q.shape[1]
    vmem = pl.BlockSpec(memory_space=pltpu.VMEM)
    hbm = pl.BlockSpec(memory_space=pl.ANY)
    dma = pltpu.SemaphoreType.DMA
    n_link, n_pass = 2 * (side + 1) * 6, 2 * side * side
    return pl.pallas_call(
        functools.partial(combine_kernel, ep, n_local),
        out_shape=jax.ShapeDtypeStruct(acc.shape, F32),
        in_specs=[hbm, hbm, vmem, vmem, vmem],
        out_specs=vmem,
        scratch_shapes=[
            pltpu.VMEM((2, side, 2, side, cap, width), BF16),
            pltpu.VMEM((2, side, 2, side, cap, width), BF16),
            pltpu.VMEM((2, 2, side, cap, width), BF16),
            pltpu.VMEM((2, side, side, 2, cap, width), BF16),
            pltpu.VMEM((2, side, 2, cap, width), BF16),
            pltpu.VMEM((2, side, side, 2, cap, width), BF16),
            pltpu.VMEM((ep, 3, tok, tok), BF16),
            dma((2,)), dma((n_link,)), dma((n_link,)), dma((n_pass,)), dma((n_pass,)),
        ],
        compiler_params=pltpu.CompilerParams(collective_id=1, has_side_effects=True, vmem_limit_bytes=VMEM_LIMIT),
        name="combine",
    )(bka, bkb, q, weights, acc)


def solution(mesh):
    ep = mesh.shape["ep"]
    tok_spec = P(("dp", "ep"))
    expert_spec = P("ep")

    def device_fn(resid_in, expert_ids, priority, norm_gain, router_w, shared_w1, shared_w3, shared_w2, expert_w1, expert_w3, expert_w2):
        n_local = expert_w1.shape[0]
        x, info, q, gates, base = dispatch(
            ep, n_local, resid_in, expert_ids, priority, norm_gain, router_w, shared_w1, shared_w3, shared_w2
        )
        e, bka, bkb = experts(ep, info, x, expert_w1, expert_w3, expert_w2)
        first = combine(ep, n_local, bka, bkb, q, gates, base)
        rounds = lax.div(info[2 * n_local, 0] + (CAP - 1), CAP)

        def one_round(carry):
            rnd, acc = carry
            more_a, more_b = fill(ep, n_local, info, rnd[None], e)
            return rnd + 1, combine(ep, n_local, more_a, more_b, q - rnd * CAP, gates, acc)

        total = lax.while_loop(lambda carry: carry[0] < rounds, one_round, (jnp.int32(1), first))[1]
        return total.astype(BF16)

    return jax.shard_map(
        device_fn, mesh=mesh,
        in_specs=(tok_spec, tok_spec, tok_spec, P(), P(), P(), P(), P(), expert_spec, expert_spec, expert_spec),
        out_specs=tok_spec, check_vma=False,
    )
```

profile of v0, /device:TPU:97, one launch (start us, length us, event | category | flops | bytes accessed | tf_op | source)
XLA Modules:
  0.0 160.0 jit_solution(5666961092010751851)
XLA Ops:
  0.0 67.2 %dispatch.1 = (bf16[896,2048]{1,0:T(8,128)(2,1)}, s32[8,128]{1,0:T(8,128)S(1)}, s32[64,128]{1,0:T(8,128)S(1)}, f32[64,128]{1,0:T(8,128)S(1)}, f32[128,2048]{1,0:T(8,128)}) custom-call(bf16[128,2048]{1,0:T(8,128)(2,1)} %y_ref.1, s32[6,128]{1,0:T(8,128)} %bitcast.10, s32[6,128]{1,0:T(8,128)} %bitcast.11, f32[1,2048]{1,0:T(1,128)} %bitcast.9, ...), custom_call_target="tpu_custom_call" | custom-call | tf_op jit(solution)/shard_map/dispatch/pallas_call | solution.py:407
  67.2 24.6 %experts.1 = (bf16[896,2048]{1,0:T(8,128)(2,1)}, bf16[4,2,4,72,512]{4,3,2,1,0:T(8,128)(2,1)}, bf16[4,2,4,72,512]{4,3,2,1,0:T(8,128)(2,1)}) custom-call(s32[8,128]{1,0:T(8,128)S(1)} %get-tuple-element.127.sc, bf16[896,2048]{1,0:T(8,128)(2,1)} %get-tuple-element.54.x_hbm, bf16[2,2048,1408]{2,1,0:T(8,128)(2,1)} %w1_hbm.1, bf16[2,2048,1408]{2,1,0:T(8,128)(2,1)} %w3_hbm.1, ...), custom_call_target="tpu_custom_call" | custom-call | tf_op jit(solution)/shard_map/experts/pallas_call | solution.py:561
  91.8 66.1 %combine.2 = f32[128,2048]{1,0:T(8,128)S(1)} custom-call(bf16[4,2,4,72,512]{4,3,2,1,0:T(8,128)(2,1)} %get-tuple-element.55.a_hbm, bf16[4,2,4,72,512]{4,3,2,1,0:T(8,128)(2,1)} %get-tuple-element.56.b_hbm, s32[64,128]{1,0:T(8,128)S(1)} %get-tuple-element.129.q_ref, f32[64,128]{1,0:T(8,128)S(1)} %get-tuple-element.130.p_ref, f32[128,2048]{1,0:T(8,128)} %get-tuple-element.59.acc_ref), custom_call_target="tpu_custom_call" | custom-call | tf_op jit(solution)/shard_map/combine/pallas_call | solution.py:815
  157.9 0.5 slice.3
  159.1 0.9 convert_element_type.3
  (1 shorter events, 0.0 us)
where the time goes:
time: 160 us
  Pallas kernels  158 us (99%)
    pallas_call x1, Pallas kernels, dispatch(): pl.pallas_call(functools.partial(dispatch_kernel, ep, top_k, n_local), ou...  67.2 us
    pallas_call x1, Pallas kernels, combine(): pl.pallas_call(functools.partial(combine_kernel, ep, n_local), out_shape=...  66.1 us
    pallas_call x1, Pallas kernels, experts(): pl.pallas_call(functools.partial(expert_kernel, ep), out_shape=(jax.Shape...  24.6 us

commit v1 on v0

--- a/solution.py
+++ b/solution.py
@@ -18,7 +18,7 @@
 SENDS = SPLIT + PAIR
 LANES = (((1,), (1,)), ((), ()))
 FAR = 1 << 20
-TILE = 128
+TILE = 64
 PARTS = ((0, 512), (512, 1024))
 AHEAD = 2
 CAP = 72
@@ -449,7 +449,7 @@
 ):
     n_local, dim, ff = w1.shape
     slots = x_ref.shape[0]
-    step = 4 * TILE
+    step = 8 * TILE
     parts = PARTS + ((PARTS[-1][1], ff),)
     last = len(parts)
     x_in = pltpu.make_async_copy(x_hbm, x_ref, x_sem)
@@ -481,7 +481,7 @@
         request(0, n)
 
     def over_tiles(first, count, body):
-        most = 4
+        most = 6
         whole = count // most
 
         def many(i):
@@ -500,7 +500,7 @@
         count = (sc[2 * l + 1, ep - 1] - sc[2 * l + 1, 0] + sc[2 * l, ep - 1] + TILE - 1) // TILE
 
         def up_cols(n):
-            start = pl.multiple_of(jnp.minimum(n * step, ff - step), TILE)
+            start = pl.multiple_of(jnp.minimum(n * step, ff - step), 2 * TILE)
             for p, (c, _) in enumerate(parts):
 
                 @pl.when(n * step == c)

time: 160 us -> 161 us (level)
  no operation moved by 1% of the time
where the time goes in v1:
time: 161 us
  Pallas kernels  159 us (99%)
    pallas_call x1, Pallas kernels, combine(): pl.pallas_call(functools.partial(combine_kernel, ep, n_local), out_shape=...  66.7 us
    pallas_call x1, Pallas kernels, dispatch(): pl.pallas_call(functools.partial(dispatch_kernel, ep, top_k, n_local), ou...  66.7 us
    pallas_call x1, Pallas kernels, experts(): pl.pallas_call(functools.partial(expert_kernel, ep), out_shape=(jax.Shape...  25.6 us

profile of v1, /device:TPU:97, one launch (start us, length us, event | category | flops | bytes accessed | tf_op | source)
XLA Modules:
  0.0 161.0 jit_solution(2671693970267309215)
XLA Ops:
  0.0 66.7 %dispatch.1 = (bf16[832,2048]{1,0:T(8,128)(2,1)}, s32[8,128]{1,0:T(8,128)S(1)}, s32[64,128]{1,0:T(8,128)S(1)}, f32[64,128]{1,0:T(8,128)S(1)}, f32[128,2048]{1,0:T(8,128)}) custom-call(bf16[128,2048]{1,0:T(8,128)(2,1)} %y_ref.1, s32[6,128]{1,0:T(8,128)} %bitcast.10, s32[6,128]{1,0:T(8,128)} %bitcast.11, f32[1,2048]{1,0:T(1,128)} %bitcast.9, ...), custom_call_target="tpu_custom_call" | custom-call | tf_op jit(solution)/shard_map/dispatch/pallas_call | solution.py:407
  66.7 25.6 %experts.1 = (bf16[832,2048]{1,0:T(8,128)(2,1)}, bf16[4,2,4,72,512]{4,3,2,1,0:T(8,128)(2,1)}, bf16[4,2,4,72,512]{4,3,2,1,0:T(8,128)(2,1)}) custom-call(s32[8,128]{1,0:T(8,128)S(1)} %get-tuple-element.127.sc, bf16[832,2048]{1,0:T(8,128)(2,1)} %get-tuple-element.54.x_hbm, bf16[2,2048,1408]{2,1,0:T(8,128)(2,1)} %w1_hbm.1, bf16[2,2048,1408]{2,1,0:T(8,128)(2,1)} %w3_hbm.1, ...), custom_call_target="tpu_custom_call" | custom-call | tf_op jit(solution)/shard_map/experts/pallas_call | solution.py:561
  92.3 66.7 %combine.2 = f32[128,2048]{1,0:T(8,128)S(1)} custom-call(bf16[4,2,4,72,512]{4,3,2,1,0:T(8,128)(2,1)} %get-tuple-element.55.a_hbm, bf16[4,2,4,72,512]{4,3,2,1,0:T(8,128)(2,1)} %get-tuple-element.56.b_hbm, s32[64,128]{1,0:T(8,128)S(1)} %get-tuple-element.129.q_ref, f32[64,128]{1,0:T(8,128)S(1)} %get-tuple-element.130.p_ref, f32[128,2048]{1,0:T(8,128)} %get-tuple-element.59.acc_ref), custom_call_target="tpu_custom_call" | custom-call | tf_op jit(solution)/shard_map/combine/pallas_call | solution.py:815
  159.0 0.5 slice.3
  160.2 0.9 convert_element_type.3
  (1 shorter events, 0.0 us)
